TPU v7x, 256 devices: a whole 4x4x8 slice. The times are simulated.
256 devices in a mesh: seq: 32 (over z, y), vocab: 8 (over x, core).
Axes of the slice: x: 4, y: 4, z: 8, core: 2. Of those that a mesh axis runs over, the one named last changes fastest.
Arguments:
- hidden: bfloat16 [3072, 3584], P('seq', 'vocab'), may hold values from -40 to 40
- lm_head: bfloat16 [3584, 152064], P(None, ('seq', 'vocab')), may hold values from -1 to 1
- positions: int32 [3072], replicated, may hold values from 0 to 3071, as said below
- vocab_limits: int32 [3072], replicated, may hold values from 76032 to 152064
- loss_mask: int32 [3072], P('seq'), may hold values 0 or 1
Outputs:
- token_entropy: float32 [3072], P('seq')
- mean_entropy: float32 [], replicated
Inputs may be any that keep to these rules, and one draw needn't show every extreme that they name: A permutation of the positions 0 to 3071: the response is cut into 64 blocks of 48 consecutive positions; rows i * 96 to i * 96 + 96 // 2 - 1 hold the positions of block i, the next 48 rows those of block 63 - i, in any order within a block.
All inputs are finite; a program needn't handle non-finite values. No bound on the sum of `loss_mask` on one device may be relied on, other than what follows from the above.
Results may differ from a plain program's by a relative error of at most 0.0003.
Values may be sent and summed in bfloat16 or wider, within the bound.
A program may use at most 128 MiB of HBM per device.

v0:
```python
import jax
import jax.numpy as jnp
from jax import lax
from jax.sharding import Mesh
from jax.sharding import PartitionSpec as P

SEQ_VOCAB = ("seq_0", "seq_1", "vocab_0", "vocab_1")
SEQ = ("seq_0", "seq_1")
VOCAB = ("vocab_0", "vocab_1")
masked_value = -1e30


def gather_axes(shard, axes, dim):
    whole = shard
    for number in range(len(axes) - 1, -1, -1):
        whole = lax.all_gather(whole, axes[number], axis=dim, tiled=True)
    return whole


def gathered_once(shard, axis):
    leaves = jax.tree.leaves(shard)
    order = sorted(range(len(leaves)), key=lambda k: -leaves[k].size)
    width = (1, *leaves[order[0]].shape)[-1]
    lines = [
        jnp.pad(leaves[k].reshape(-1), (0, -leaves[k].size % width)).reshape(-1, width)
        for k in order
    ]
    both, at, found = (lax.all_gather(jnp.concatenate(lines), axis), 0, {})
    for k, line in zip(order, lines):
        section = both[:, at : at + len(line)].reshape(len(both), -1)
        found[k] = section[:, : leaves[k].size].reshape(-1, *leaves[k].shape)
        at += len(line)
    numbers = iter(range(len(leaves)))
    return jax.tree.map(lambda _: found[next(numbers)], shard)


def combined_by_axis(shard, axes, combine):
    for axis in axes:
        pieces = gathered_once(shard, axis)
        shard = jax.tree.map(lambda part: part[0], pieces)
        for k in range(1, lax.axis_size(axis)):
            shard = combine(shard, jax.tree.map(lambda part: part[k], pieces))
    return shard


def copy_for_each(shard, axis):
    copies = jnp.broadcast_to(shard, (lax.axis_size(axis), *shard.shape))
    return lax.all_to_all(copies, axis, split_axis=0, concat_axis=0, tiled=True)


def taken_together(shard, axis):
    everything = copy_for_each(shard, axis)
    return jnp.sum(everything, axis=0)


def together(arrays, axis):
    flat, at, finished = (jnp.concatenate([a.reshape(-1) for a in arrays]), 0, [])
    total = taken_together(flat, axis)
    for a in arrays:
        finished.append(total[at : at + a.size].reshape(a.shape))
        at += a.size
    return tuple(finished)


def row_stats(logits, row_limits, first_column):
    columns = first_column + lax.iota(jnp.int32, logits.shape[1])
    allowed = columns[None, :] < row_limits[:, None]
    row_peak = jnp.max(jnp.where(allowed, logits, masked_value), axis=1)
    shifted = logits - row_peak[:, None]
    weights = jnp.where(allowed, jnp.exp(shifted), 0.0)
    row_total = jnp.sum(weights, axis=1)
    row_moment = jnp.sum(weights * jnp.where(allowed, shifted, 0.0), axis=1)
    return (row_peak, row_total, row_moment)


def combine_stats(first, second):
    peak_one, total_one, moment_one = first
    peak_two, total_two, moment_two = second
    shared = jnp.maximum(peak_one, peak_two)
    ratio_one = jnp.exp(peak_one - shared)
    ratio_two = jnp.exp(peak_two - shared)
    total = ratio_one * total_one + ratio_two * total_two
    moment = ratio_one * (moment_one + total_one * (peak_one - shared)) + ratio_two * (
        moment_two + total_two * (peak_two - shared)
    )
    return (shared, total, moment)


def local(hidden, lm_head, positions, vocab_limits, loss_mask):
    tok_dev = hidden.shape[0]
    width_dev = lm_head.shape[1]
    tokens_all = positions.shape[0]
    first_column = lax.axis_index(SEQ_VOCAB) * width_dev
    all_tokens = gather_axes(hidden, SEQ, 0)
    logits = jnp.dot(
        lax.all_gather(all_tokens, VOCAB, axis=1, tiled=True),
        lm_head,
        preferred_element_type=jnp.float32,
    )
    stats = row_stats(logits, vocab_limits, first_column)
    own_start = lax.axis_index(SEQ) * tok_dev
    row_peak, row_total, row_moment = combined_by_axis(stats, SEQ_VOCAB, combine_stats)
    entropy_rows = jnp.log(row_total) - row_moment / row_total
    arranged = jnp.zeros((tokens_all,), jnp.float32).at[positions].set(entropy_rows)
    token_entropy = lax.dynamic_slice_in_dim(arranged, own_start, tok_dev)
    mask_float = loss_mask.astype(jnp.float32)
    masked_sum, mask_count = together(
        (jnp.sum(token_entropy * mask_float), jnp.sum(mask_float)), SEQ
    )
    mean_entropy = masked_sum / jnp.maximum(mask_count, 1.0)
    return (token_entropy, mean_entropy)


def solution(mesh):
    torus = Mesh(mesh.devices.reshape(8, 4, 4, 2), ("seq_0", "seq_1", "vocab_0", "vocab_1"))
    in_specs = (P(SEQ, VOCAB), P(None, SEQ_VOCAB), P(), P(), P(SEQ))
    out_specs = (P(SEQ), P())
    return jax.shard_map(local, mesh=torus, in_specs=in_specs, out_specs=out_specs, check_vma=False)
```

profile of v0, /device:TPU:1, one launch (start us, length us, event | category | flops | bytes accessed | tf_op | source)
XLA Modules:
  0.0 298.8 jit_solution(5486878715596462331)
XLA Ops:
  7.2 0.0 copy-start.1
  7.2 0.0 all-gather.11.cloned.1.call-start
  7.2 13.0 %all_gather.33 = bf16[384,448]{1,0:T(8,128)(2,1)} all-gather(bf16[96,448]{1,0:T(8,128)(2,1)} %param.5), channel_id=1, replica_groups=mesh['seq_0'=8,'seq_1'=4,'vocab_0'=4,'vocab_1'=2] {'seq_1'}, dimensions={0}, use_global_device_ids=true | all-gather | bytes 430080 | tf_op jit(solution)/shard_map/all_gather | solution.py:16
  20.2 0.0 all-gather.11.cloned.1.call-update
  20.3 0.0 all-gather.13.cloned.1.call-start
  20.3 48.6 %all-gather.11.cloned.1.call-done = bf16[3072,448]{1,0:T(8,128)(2,1)} async-done(((bf16[384,448]{1,0:T(8,128)(2,1)}), bf16[3072,448]{1,0:T(8,128)(2,1)}) %all-gather.11.cloned.1.call-update) | async-done | bytes 2752528 | tf_op jit(solution)/shard_map/all_gather | solution.py:16
  68.9 4.6 %copy.10 = bf16[3072,448]{0,1:T(8,128)(2,1)} copy(bf16[3072,448]{1,0:T(8,128)(2,1)} %all-gather.11.cloned.1.call-done) | data formatting | bytes 5505024 | tf_op jit(solution)/shard_map/all_gather | solution.py:16
  73.5 0.0 all-gather.13.cloned.1.call-update
  73.6 0.0 copy-done.1
  73.6 109.1 %all-gather.13.cloned.1.call-done = bf16[3072,3584]{0,1:T(8,128)(2,1)} async-done(((bf16[3072,448]{0,1:T(8,128)(2,1)}), bf16[3072,3584]{0,1:T(8,128)(2,1)}) %all-gather.13.cloned.1.call-update) | async-done | bytes 22020112 | tf_op jit(solution)/shard_map/all_gather | solution.py:96
  182.8 0.0 copy-done
  182.8 18.4 %fusion = (f32[3072]{0:T(1024)S(1)}, f32[3072,594]{0,1:T(8,128)S(1)}) fusion(s32[3072]{0:T(1024)S(1)} %copy-done, s32[594]{0:T(1024)S(1)} %iota_add_fusion, bf16[3072,3584]{0,1:T(8,128)(2,1)} %all-gather.13.cloned.1.call-done, bf16[3584,594]{0,1:T(8,128)(2,1)} %param.6), kind=kOutput, calls=%fused_computation.4 | convolution fusion | flops 13085408256 | bytes 33603912 | tf_op jit(solution)/shard_map/dot_general | solution.py:95
  201.2 0.0 copy-start.2
  201.2 2.5 fusion.3
  203.8 20.1 %all-gather.4 = f32[8,3,3072]{2,1,0:T(4,128)S(1)} all-gather(f32[1,3,3072]{2,1,0:T(4,128)S(1)} %maximum_bitcast_fusion), channel_id=2, replica_groups=mesh['seq_0'=8,'seq_1'=4,'vocab_0'=4,'vocab_1'=2] {'seq_0'}, dimensions={0}, use_global_device_ids=true | all-gather | bytes 331776 | tf_op jit(solution)/shard_map/all_gather | solution.py:28
  223.9 0.1 fusion.63
  224.0 0.3 multiply_add_fusion.6
  224.3 0.5 fusion.28
  224.8 9.9 %all-gather.5 = f32[4,3,3072]{2,1,0:T(4,128)S(1)} all-gather(f32[1,3,3072]{2,1,0:T(4,128)S(1)} %maximum_bitcast_fusion.1), channel_id=3, replica_groups=mesh['seq_0'=8,'seq_1'=4,'vocab_0'=4,'vocab_1'=2] {'seq_1'}, dimensions={0}, use_global_device_ids=true | all-gather | bytes 184320 | tf_op jit(solution)/shard_map/all_gather | solution.py:28
  234.6 0.1 fusion.70
  234.8 0.2 fusion.17
  235.0 9.2 %all-gather.6 = f32[4,3,3072]{2,1,0:T(4,128)S(1)} all-gather(f32[1,3,3072]{2,1,0:T(4,128)S(1)} %maximum_bitcast_fusion.2), channel_id=4, replica_groups=mesh['seq_0'=8,'seq_1'=4,'vocab_0'=4,'vocab_1'=2] {'vocab_0'}, dimensions={0}, use_global_device_ids=true | all-gather | bytes 184320 | tf_op jit(solution)/shard_map/all_gather | solution.py:28
  244.3 0.1 fusion.77
  244.4 0.2 fusion.6
  244.7 13.7 %all-gather.7 = f32[2,3,3072]{2,1,0:T(4,128)S(1)} all-gather(f32[1,3,3072]{2,1,0:T(4,128)S(1)} %maximum_bitcast_fusion.3), channel_id=5, replica_groups=mesh['seq_0'=8,'seq_1'=4,'vocab_0'=4,'vocab_1'=2] {'vocab_1'}, dimensions={0}, use_global_device_ids=true | all-gather | bytes 110592 | tf_op jit(solution)/shard_map/all_gather | solution.py:28
  258.4 0.1 fusion.82
  258.5 11.8 %scatter_custom_fusion = f32[3072]{0:T(1024)S(1)} fusion(s32[3072]{0:T(1024)S(1)} %compare_select_fusion.3, f32[3072]{0:T(1024)S(1)} %divide_subtract_fusion, f32[]{:T(128)} %constant.16.clone.1), kind=kCustom, calls=%fused_computation.151 | custom fusion | bytes 12292 | tf_op jit(solution)/shard_map/scatter | solution.py:104
  270.3 1.3 multiply_reduce_fusion
  271.5 1.4 pad_maximum_fusion
  273.0 15.9 %all_to_all.6 = f32[32,1,2]{2,1,0:T(1,128)S(1)} all-to-all(f32[32,1,2]{2,1,0:T(1,128)S(1)} %broadcast_in_dim.24), channel_id=1, replica_groups=mesh['seq_0'=8,'seq_1'=4,'vocab_0'=4,'vocab_1'=2] {'seq_0','seq_1'}, dimensions={0} | all-to-all | bytes 512 | tf_op jit(solution)/shard_map/all_to_all | solution.py:48
  288.8 0.1 reduce_sum.49
  288.9 0.6 fusion.83
  (10 shorter events, 0.2 us)
Async XLA Ops:
  7.2 66.4 %copy-start.1 = (s32[3072]{0:T(1024)S(1)}, s32[3072]{0:T(1024)}, u32[]{:S(2)}) copy-start(s32[3072]{0:T(1024)} %param.7) | copy-start | bytes 36868
  7.2 175.6 %copy-start = (s32[3072]{0:T(1024)S(1)}, s32[3072]{0:T(1024)}, u32[]{:S(2)}) copy-start(s32[3072]{0:T(1024)} %param.8) | copy-start | bytes 36868
  7.2 61.7 %all-gather.11.cloned.1.call-start = ((), (), s32[]{:S(2)}) async-start(), calls=%async_computation.1 | async-start | bytes 3538944 | tf_op jit(solution)/shard_map/all_gather | solution.py:16
  20.3 162.5 %all-gather.13.cloned.1.call-start = ((), (), s32[]{:S(2)}) async-start(), calls=%async_computation.2 | async-start | bytes 24772608 | tf_op jit(solution)/shard_map/all_gather | solution.py:96
  201.2 69.1 %copy-start.2 = (s32[96]{0:T(128)S(1)}, s32[96]{0:T(128)}, u32[]{:S(2)}) copy-start(s32[96]{0:T(128)} %param.9) | copy-start | bytes 1156
Sparse Core Ops, SparseCore 0:
  20.4 48.4 all-gather.10
  73.7 109.0 all-gather.12
where the time goes:
time: 299 us
  waiting for transfers between devices  158 us (53%)
  blocking collectives  81.8 us (27%)
  matrix products  18.4 us (6%)
  local copies, waits for them, and re-layouts  17.1 us (6%)
  between operations  16.7 us (6%)
  other arithmetic  6.95 us (2%)
    all_gather x1, waiting for transfers between devices, local(): lax.all_gather(all_tokens, VOCAB, axis=1, tiled=True)  109 us
    all_gather x4, blocking collectives, gathered_once(): both, at, found = (lax.all_gather(jnp.concatenate(lines), axis), 0, {})  53 us
    all_gather x1, waiting for transfers between devices, gather_axes(): whole = lax.all_gather(whole, axes[number], axis=dim, tiled=True)  48.6 us
    dot_general x1, matrix products, local(): jnp.dot(lax.all_gather(all_tokens, VOCAB, axis=1, tiled=True), lm_head, p...  18.4 us
    all_to_all x1, blocking collectives, copy_for_each(): return lax.all_to_all(copies, axis, split_axis=0, concat_axis=0, tiled=True)  15.9 us
    all_gather x1, blocking collectives, gather_axes(): whole = lax.all_gather(whole, axes[number], axis=dim, tiled=True)  13 us
    scatter x1, local copies, waits for them, and re-layouts, local(): jnp.zeros((tokens_all,), jnp.float32).at[positions].set(entropy_rows)  11.8 us
  transfers between devices with their start and end apart: 2, of which 2 were waited for; matrix products, arithmetic and copies ran while one was open for 0% of the time, Pallas kernels for 0%

commit v1 on v0

--- a/solution.py
+++ b/solution.py
@@ -8,6 +8,13 @@
 SEQ = ("seq_0", "seq_1")
 VOCAB = ("vocab_0", "vocab_1")
 masked_value = -1e30
+
+
+def swapped_in(x, mesh_axis, along):
+    size = lax.axis_size(mesh_axis)
+    tiles = jnp.stack([x for _ in range(size)])
+    tiles = lax.all_to_all(tiles, mesh_axis, split_axis=0, concat_axis=0)
+    return jnp.concatenate(tiles, axis=along)
 
 
 def gather_axes(shard, axes, dim):
@@ -92,11 +99,7 @@
     tokens_all = positions.shape[0]
     first_column = lax.axis_index(SEQ_VOCAB) * width_dev
     all_tokens = gather_axes(hidden, SEQ, 0)
-    logits = jnp.dot(
-        lax.all_gather(all_tokens, VOCAB, axis=1, tiled=True),
-        lm_head,
-        preferred_element_type=jnp.float32,
-    )
+    logits = jnp.dot(swapped_in(all_tokens, VOCAB, 1), lm_head, preferred_element_type=jnp.float32)
     stats = row_stats(logits, vocab_limits, first_column)
     own_start = lax.axis_index(SEQ) * tok_dev
     row_peak, row_total, row_moment = combined_by_axis(stats, SEQ_VOCAB, combine_stats)

time: 299 us -> 442 us (1.48)
  waiting for transfers between devices: 158 us -> 288 us
  starting transfers between devices: 0.08 us -> 7.48 us
  local copies, waits for them, and re-layouts: 17.1 us -> 23.3 us
    all_to_all x0 -> x1, waiting for transfers between devices: none -> 240 us  [swapped_in(): tiles = lax.all_to_all(tiles, mesh_axis, split_axis=0, concat_axis=0)]
    all_gather x1 -> x0, waiting for transfers between devices: 109 us -> none  [local(): lax.all_gather(all_tokens, VOCAB, axis=1, tiled=True)]
    another operation x0 -> x1, local copies, waits for them, and re-layouts: none -> 7.72 us  [swapped_in(): tiles = jnp.stack([x for _ in range(size)])]
    all_to_all x0 -> x1, starting transfers between devices: none -> 7.44 us  [swapped_in(): tiles = lax.all_to_all(tiles, mesh_axis, split_axis=0, concat_axis=0)]
where the time goes in v1:
time: 442 us
  waiting for transfers between devices  288 us (65%)
  blocking collectives  80 us (18%)
  local copies, waits for them, and re-layouts  23.3 us (5%)
  matrix products  18.8 us (4%)
  between operations  16.6 us (4%)
  starting transfers between devices  7.48 us (2%)
  other arithmetic  6.95 us (2%)
    all_to_all x1, waiting for transfers between devices, swapped_in(): tiles = lax.all_to_all(tiles, mesh_axis, split_axis=0, concat_axis=0)  240 us
    all_gather x4, blocking collectives, gathered_once(): both, at, found = (lax.all_gather(jnp.concatenate(lines), axis), 0, {})  52.2 us
    all_gather x1, waiting for transfers between devices, gather_axes(): whole = lax.all_gather(whole, axes[number], axis=dim, tiled=True)  48.7 us
    dot_general x1, matrix products, local(): jnp.dot(swapped_in(all_tokens, VOCAB, 1), lm_head, preferred_element_type...  18.8 us
    all_to_all x1, blocking collectives, copy_for_each(): return lax.all_to_all(copies, axis, split_axis=0, concat_axis=0, tiled=True)  14.9 us
    all_gather x1, blocking collectives, gather_axes(): whole = lax.all_gather(whole, axes[number], axis=dim, tiled=True)  13 us
    scatter x1, local copies, waits for them, and re-layouts, local(): jnp.zeros((tokens_all,), jnp.float32).at[positions].set(entropy_rows)  11.8 us
  transfers between devices with their start and end apart: 2, of which 2 were waited for; matrix products, arithmetic and copies ran while one was open for 0% of the time, Pallas kernels for 0%

profile of v1, /device:TPU:1, one launch (start us, length us, event | category | flops | bytes accessed | tf_op | source)
XLA Modules:
  0.0 441.6 jit_solution(15966979080843063210)
XLA Ops:
  7.2 0.0 all-gather.10.cloned.1.call-start
  7.2 13.0 %all_gather.30 = bf16[384,448]{1,0:T(8,128)(2,1)} all-gather(bf16[96,448]{1,0:T(8,128)(2,1)} %param.5), channel_id=1, replica_groups=mesh['seq_0'=8,'seq_1'=4,'vocab_0'=4,'vocab_1'=2] {'seq_1'}, dimensions={0}, use_global_device_ids=true | all-gather | bytes 430080 | tf_op jit(solution)/shard_map/all_gather | solution.py:23
  20.2 0.0 all-gather.10.cloned.1.call-update
  20.2 48.7 %all-gather.10.cloned.1.call-done = bf16[3072,448]{1,0:T(8,128)(2,1)} async-done(((bf16[384,448]{1,0:T(8,128)(2,1)}), bf16[3072,448]{1,0:T(8,128)(2,1)}) %all-gather.10.cloned.1.call-update) | async-done | bytes 2752528 | tf_op jit(solution)/shard_map/all_gather | solution.py:23
  68.9 3.1 copy.10
  72.0 7.7 %stack.2 = bf16[8,3072,448]{1,2,0:T(8,128)(2,1)} broadcast(bf16[3072,448]{0,1:T(8,128)(2,1)S(1)} %copy.10), dimensions={1,2} | broadcast | bytes 24772608 | tf_op jit(solution)/shard_map/stack | solution.py:15
  79.7 7.4 %all-to-all-start = ((bf16[8,3072,448]{1,2,0:T(8,128)(2,1)}), bf16[8,3072,448]{1,2,0:T(8,128)(2,1)}, u32[]{:S(2)}, u32[]{:S(2)}) async-start(bf16[8,3072,448]{1,2,0:T(8,128)(2,1)} %stack.2), calls=%async_computation | async-start | bytes 44040192 | tf_op jit(solution)/shard_map/all_to_all | solution.py:16
  87.2 0.0 copy-done.1
  87.2 239.8 %all-to-all-done = bf16[8,3072,448]{1,2,0:T(8,128)(2,1)} async-done(((bf16[8,3072,448]{1,2,0:T(8,128)(2,1)}), bf16[8,3072,448]{1,2,0:T(8,128)(2,1)}, u32[]{:S(2)}, u32[]{:S(2)}) %all-to-all-start) | async-done | bytes 22020128 | tf_op jit(solution)/shard_map/all_to_all | solution.py:16
  327.0 0.0 copy-done
  327.0 18.8 %fusion = (f32[3072]{0:T(1024)S(1)}, f32[3072,594]{0,1:T(8,128)S(1)}) fusion(s32[3072]{0:T(1024)S(1)} %copy-done, s32[594]{0:T(1024)S(1)} %iota_add_fusion, bf16[3072,3584]{0,1:T(8,128)(2,1)} %bitcast.1, bf16[3584,594]{0,1:T(8,128)(2,1)} %param.6), kind=kOutput, calls=%fused_computation.4 | convolution fusion | flops 13085408256 | bytes 33603912 | tf_op jit(solution)/shard_map/dot_general | solution.py:102
  345.8 0.0 copy-start.2
  345.8 2.6 fusion.3
  348.4 19.0 %all-gather.4 = f32[8,3,3072]{2,1,0:T(4,128)S(1)} all-gather(f32[1,3,3072]{2,1,0:T(4,128)S(1)} %maximum_bitcast_fusion), channel_id=2, replica_groups=mesh['seq_0'=8,'seq_1'=4,'vocab_0'=4,'vocab_1'=2] {'seq_0'}, dimensions={0}, use_global_device_ids=true | all-gather | bytes 331776 | tf_op jit(solution)/shard_map/all_gather | solution.py:35
  367.4 0.1 fusion.63
  367.5 0.3 multiply_add_fusion.6
  367.7 0.5 fusion.28
  368.3 9.6 %all-gather.5 = f32[4,3,3072]{2,1,0:T(4,128)S(1)} all-gather(f32[1,3,3072]{2,1,0:T(4,128)S(1)} %maximum_bitcast_fusion.1), channel_id=3, replica_groups=mesh['seq_0'=8,'seq_1'=4,'vocab_0'=4,'vocab_1'=2] {'seq_1'}, dimensions={0}, use_global_device_ids=true | all-gather | bytes 184320 | tf_op jit(solution)/shard_map/all_gather | solution.py:35
  377.8 0.1 fusion.70
  378.0 0.2 fusion.17
  378.2 9.2 %all-gather.6 = f32[4,3,3072]{2,1,0:T(4,128)S(1)} all-gather(f32[1,3,3072]{2,1,0:T(4,128)S(1)} %maximum_bitcast_fusion.2), channel_id=4, replica_groups=mesh['seq_0'=8,'seq_1'=4,'vocab_0'=4,'vocab_1'=2] {'vocab_0'}, dimensions={0}, use_global_device_ids=true | all-gather | bytes 184320 | tf_op jit(solution)/shard_map/all_gather | solution.py:35
  387.5 0.1 fusion.77
  387.6 0.2 fusion.6
  387.9 14.3 %all-gather.7 = f32[2,3,3072]{2,1,0:T(4,128)S(1)} all-gather(f32[1,3,3072]{2,1,0:T(4,128)S(1)} %maximum_bitcast_fusion.3), channel_id=5, replica_groups=mesh['seq_0'=8,'seq_1'=4,'vocab_0'=4,'vocab_1'=2] {'vocab_1'}, dimensions={0}, use_global_device_ids=true | all-gather | bytes 110592 | tf_op jit(solution)/shard_map/all_gather | solution.py:35
  402.2 0.1 fusion.82
  402.3 11.8 %scatter_custom_fusion = f32[3072]{0:T(1024)S(1)} fusion(s32[3072]{0:T(1024)S(1)} %compare_select_fusion.3, f32[3072]{0:T(1024)S(1)} %divide_subtract_fusion, f32[]{:T(128)} %constant.16.clone.1), kind=kCustom, calls=%fused_computation.151 | custom fusion | bytes 12292 | tf_op jit(solution)/shard_map/scatter | solution.py:107
  414.1 0.0 copy-done.2
  414.1 1.3 multiply_reduce_fusion
  415.4 1.4 pad_maximum_fusion
  416.8 14.9 %all_to_all.11 = f32[32,1,2]{2,1,0:T(1,128)S(1)} all-to-all(f32[32,1,2]{2,1,0:T(1,128)S(1)} %broadcast_in_dim.24), channel_id=1, replica_groups=mesh['seq_0'=8,'seq_1'=4,'vocab_0'=4,'vocab_1'=2] {'seq_0','seq_1'}, dimensions={0} | all-to-all | bytes 512 | tf_op jit(solution)/shard_map/all_to_all | solution.py:55
  431.7 0.1 reduce_sum.49
  431.7 0.6 fusion.83
  (10 shorter events, 0.2 us)
Async XLA Ops:
  7.2 61.7 %all-gather.10.cloned.1.call-start = ((), (), s32[]{:S(2)}) async-start(), calls=%async_computation.2 | async-start | bytes 3538944 | tf_op jit(solution)/shard_map/all_gather | solution.py:23
  79.7 7.5 %copy-start.1 = (s32[3072]{0:T(1024)S(1)}, s32[3072]{0:T(1024)}, u32[]{:S(2)}) copy-start(s32[3072]{0:T(1024)} %param.7) | copy-start | bytes 36868
  79.7 247.3 %copy-start = (s32[3072]{0:T(1024)S(1)}, s32[3072]{0:T(1024)}, u32[]{:S(2)}) copy-start(s32[3072]{0:T(1024)} %param.8) | copy-start | bytes 36868
  79.7 247.3 %all-to-all-start = ((bf16[8,3072,448]{1,2,0:T(8,128)(2,1)}), bf16[8,3072,448]{1,2,0:T(8,128)(2,1)}, u32[]{:S(2)}, u32[]{:S(2)}) async-start(bf16[8,3072,448]{1,2,0:T(8,128)(2,1)} %stack.2), calls=%async_computation | async-start | bytes 44040192 | tf_op jit(solution)/shard_map/all_to_all | solution.py:16
  345.8 68.3 %copy-start.2 = (s32[96]{0:T(128)S(1)}, s32[96]{0:T(128)}, u32[]{:S(2)}) copy-start(s32[96]{0:T(128)} %param.9) | copy-start | bytes 1156
Sparse Core Ops, SparseCore 0:
  20.4 48.4 all-gather.9
